TPU v7x, 32 devices: a whole 2x2x4 slice. The times are simulated.
32 devices in a mesh: expert: 8 (over y, x, core), replica: 4 (over z).
Axes of the slice: x: 2, y: 2, z: 4, core: 2. Of those that a mesh axis runs over, the one named last changes fastest.
Arguments:
- tokens_in: bfloat16 [8192, 2048], P(('expert', 'replica')), may hold values from -6 to 6
- cotangents: bfloat16 [8192, 8192], P(('expert', 'replica')), may hold values from -0.1796875 to 0.1796875
- left_root: bfloat16 [8, 2048, 2048], P('expert'), may hold values from -2 to 6, as said below
- right_root: bfloat16 [8, 8, 1024, 1024], P('expert', 'replica'), may hold values from -2 to 6, as said below
Outputs:
- update: bfloat16 [8, 2048, 8192], P('expert', None, 'replica')
Inputs may be any that keep to these rules, and one draw needn't show every extreme that they name: `left_root`: each matrix is symmetric. `right_root`: each block is symmetric.
All inputs are finite; a program needn't handle non-finite values.
Results may differ from a plain program's by a relative error of at most 0.0058.
Values may be sent and summed in bfloat16 or wider, within the bound.
A program may use at most 192 MiB of HBM per device.

v0:
```python
import functools
import jax
import jax.numpy as jnp
from jax import lax
from jax.experimental import pallas as pl
from jax.experimental.pallas import tpu as pltpu
from jax.sharding import PartitionSpec as P


def tile_of(size, most):
    return most if size % most == 0 else size


def route_kernel(
    ne, nr, tok_ref, cot_ref, left_ref, right_ref, x_ref, y_ref,
    tok, cot, left, right, x, y,
    plane_send, up_send, down_send, tok_recv, cot_send, cot_recv, local,
):
    e = lax.axis_index("expert")
    r = lax.axis_index("replica")
    rows = tok_ref.shape[0] // ne
    group = rows * ne
    width = tok.shape[1]
    cols = cot.shape[1]
    blocks, order = right_ref.shape[0], right_ref.shape[1]

    load_left = pltpu.make_async_copy(left_ref, left, local.at[0])
    load_right = pltpu.make_async_copy(right_ref, right, local.at[1])
    load_left.start()
    load_right.start()

    barrier = pltpu.get_barrier_semaphore()

    @pl.loop(1, ne * nr)
    def _(k):
        pl.semaphore_signal(
            barrier, inc=1,
            device_id={"expert": (e + k % ne) % ne, "replica": (r + k // ne) % nr},
        )

    pl.semaphore_wait(barrier, ne * nr - 1)

    def span(origin, source):
        return pl.ds(pl.multiple_of((origin * ne + source) * rows, rows), rows)

    def own_rows(target):
        return pl.ds(pl.multiple_of(target * rows, rows), rows)

    def own_cols(target):
        return pl.ds(pl.multiple_of(target * cols, cols), cols)

    def plane_copy(target):
        return pltpu.make_async_remote_copy(
            tok_ref.at[own_rows(target)], tok.at[span(r, e)],
            plane_send.at[target], tok_recv.at[r * ne + e],
            device_id={"expert": target, "replica": r},
        )

    def relay(origin, source, up):
        at = span(origin, source)
        k = origin * ne + source
        return pltpu.make_async_remote_copy(
            tok.at[at], tok.at[at],
            (up_send if up else down_send).at[k], tok_recv.at[k],
            device_id={"expert": e, "replica": r + 1 if up else r - 1},
        )

    def tok_wait(origin, source):
        pltpu.make_async_remote_copy(
            tok.at[span(origin, source)], tok.at[span(origin, source)],
            up_send.at[0], tok_recv.at[origin * ne + source],
            device_id={"expert": e, "replica": (r + 1) % nr},
        ).wait_recv()

    def cot_copy(te, tr):
        return pltpu.make_async_remote_copy(
            cot_ref.at[own_rows(te), own_cols(tr)], cot.at[span(r, e)],
            cot_send.at[tr * ne + te], cot_recv.at[r * ne + e],
            device_id={"expert": te, "replica": tr},
        )

    def send_cots(te, distance):
        for tr in (r + distance, r - distance):
            @pl.when((tr >= 0) & (tr < nr))
            def _():
                cot_copy(te, tr).start()

    def forward(origin, source, up):
        ahead = (r + 1 < nr) if up else (r > 0)

        @pl.when(ahead)
        def _():
            relay(origin, source, up).start()

    own_tok = pltpu.make_async_copy(tok_ref.at[own_rows(e)], tok.at[span(r, e)], local.at[2])
    own_cot = pltpu.make_async_copy(cot_ref.at[own_rows(e), own_cols(r)], cot.at[span(r, e)], local.at[3])
    own_tok.start()
    own_cot.start()

    @pl.loop(1, ne)
    def _(k):
        plane_copy((e + k) % ne).start()

    own_tok.wait()

    @pl.loop(0, ne)
    def _(k):
        source = (e + ne - k) % ne

        @pl.when(k > 0)
        def _():
            tok_wait(r, source)

        forward(r, source, True)
        forward(r, source, False)
        for distance in range(nr - 1, 1, -1):
            send_cots((e + k) % ne, distance)

    step = tile_of(width, 256)

    def make_x(g):
        columns = pl.ds(pl.multiple_of(g * group, group), group)

        @pl.loop(0, width // step)
        def _(i):
            part = pl.ds(pl.multiple_of(i * step, step), step)
            x[part, columns] = lax.dot_general(
                left[part, :], tok[columns, :], (((1,), (1,)), ((), ())),
                preferred_element_type=jnp.float32,
            ).astype(x.dtype)

    for distance in range(1, nr):
        @pl.loop(0, ne)
        def _(k):
            source = (e + ne - k) % ne

            @pl.when(r - distance >= 0)
            def _():
                tok_wait(r - distance, source)
                forward(r - distance, source, True)

            @pl.when(r + distance < nr)
            def _():
                tok_wait(r + distance, source)
                forward(r + distance, source, False)

            if distance == 1:
                send_cots((e + k) % ne, 1)

                @pl.when(k > 0)
                def _():
                    cot_copy((e + k) % ne, r).start()

        if distance == 1:
            load_left.wait()
            make_x(r)
        for g in (r - distance, r + distance):
            @pl.when((g >= 0) & (g < nr))
            def _():
                make_x(g)

    store_x = pltpu.make_async_copy(x, x_ref, local.at[2])
    store_x.start()
    load_right.wait()
    own_cot.wait()

    def store_y(g):
        at = pl.ds(pl.multiple_of(g * group, group), group)
        return pltpu.make_async_copy(y.at[at], y_ref.at[at], local.at[4 + g])

    @pl.loop(0, nr)
    def _(i):
        g = (r + nr // 2 + i) % nr

        @pl.loop(0, ne)
        def _(s):
            @pl.when((s != e) | (g != r))
            def _():
                pltpu.make_async_remote_copy(
                    cot_ref.at[own_rows(s), own_cols(g)], cot.at[span(g, s)],
                    cot_send.at[0], cot_recv.at[g * ne + s],
                    device_id={"expert": (e + 1) % ne, "replica": r},
                ).wait_recv()

        at = pl.ds(pl.multiple_of(g * group, group), group)
        for b in range(blocks):
            inside = slice(b * order, (b + 1) * order)
            y[at, inside] = jnp.dot(
                cot[at, inside], right[b], preferred_element_type=jnp.float32
            ).astype(y.dtype)
        store_y(g).start()

    @pl.loop(1, ne)
    def _(k):
        plane_copy((e + k) % ne).wait_send()

    @pl.loop(0, ne * nr)
    def _(k):
        tr, te = k // ne, k % ne

        @pl.when((te != e) | (tr != r))
        def _():
            cot_copy(te, tr).wait_send()

        @pl.when((tr <= r) & (r + 1 < nr))
        def _():
            relay(tr, te, True).wait_send()

        @pl.when((tr >= r) & (r > 0))
        def _():
            relay(tr, te, False).wait_send()

    store_x.wait()

    @pl.loop(0, nr)
    def _(g):
        store_y(g).wait()


def body(tokens_in, cotangents, left_root, right_root):
    ne, nr = lax.axis_size("expert"), lax.axis_size("replica")
    assert left_root.shape[0] == 1
    width = tokens_in.shape[1]
    columns = cotangents.shape[1] // nr
    total = tokens_in.shape[0] * nr
    blocks, order = right_root.shape[1], right_root.shape[2]
    anywhere = pl.BlockSpec(memory_space=pl.ANY)
    n = ne * nr
    dtype = jnp.bfloat16
    dma = pltpu.SemaphoreType.DMA
    x, y = pl.pallas_call(
        functools.partial(route_kernel, ne, nr),
        out_shape=[
            jax.ShapeDtypeStruct((width, total), dtype),
            jax.ShapeDtypeStruct((total, columns), dtype),
        ],
        in_specs=[anywhere] * 4,
        out_specs=[anywhere] * 2,
        scratch_shapes=[
            pltpu.VMEM((total, width), dtype),
            pltpu.VMEM((total, columns), dtype),
            pltpu.VMEM((width, width), dtype),
            pltpu.VMEM((blocks, order, order), dtype),
            pltpu.VMEM((width, total), dtype),
            pltpu.VMEM((total, columns), dtype),
            dma((ne,)), dma((n,)), dma((n,)), dma((n,)), dma((n,)), dma((n,)), dma((4 + nr,)),
        ],
        compiler_params=pltpu.CompilerParams(collective_id=0, has_side_effects=True),
    )(tokens_in, cotangents, left_root[0], right_root[0])
    return jnp.dot(x, y, preferred_element_type=jnp.float32).astype(dtype)[None]


def solution(mesh):
    in_specs = (
        P(("expert", "replica"), None),
        P(("expert", "replica"), None),
        P("expert", None, None),
        P("expert", "replica", None, None),
    )
    out_specs = P("expert", None, "replica")
    return jax.shard_map(body, mesh=mesh, in_specs=in_specs, out_specs=out_specs, check_vma=False)
```

profile of v0, /device:TPU:1, one launch (start us, length us, event | category | flops | bytes accessed | tf_op | source)
XLA Modules:
  0.0 169.4 jit_solution(7608650627281876234)
XLA Ops:
  0.0 155.5 %shard_map.46 = (bf16[2048,1024]{1,0:T(8,128)(2,1)}, bf16[1024,2048]{1,0:T(8,128)(2,1)}) custom-call(bf16[256,2048]{1,0:T(8,128)(2,1)} %tok_ref.1, bf16[256,8192]{1,0:T(8,128)(2,1)} %cot_ref.1, bf16[2048,2048]{1,0:T(8,128)(2,1)} %bitcast.6, bf16[2,1024,1024]{2,1,0:T(8,128)(2,1)} %bitcast.7), custom_call_target="tpu_custom_call" | custom-call | tf_op jit(solution)/shard_map/pallas_call | solution.py:231
  155.5 13.9 %convert_bitcast_fusion = bf16[1,2048,2048]{2,1,0:T(8,128)(2,1)} fusion(bf16[2048,1024]{1,0:T(8,128)(2,1)} %get-tuple-element.7, bf16[1024,2048]{1,0:T(8,128)(2,1)} %get-tuple-element.8), kind=kOutput, calls=%fused_computation | convolution fusion | flops 8594128896 | bytes 16777216 | tf_op jit(solution)/shard_map/dot_general | solution.py:250
where the time goes:
time: 172 us; the launch traced here: 169 us
  Pallas kernels  155 us (90%)
  matrix products  13.9 us (8%)
    pallas_call x1, Pallas kernels, body(): pl.pallas_call(functools.partial(route_kernel, ne, nr), out_shape=[jax.Sh...  155 us
    dot_general x1, matrix products, body(): return jnp.dot(x, y, preferred_element_type=jnp.float32).astype(dtype)[None]  13.9 us

commit v1 on v0

v1 whole, which is shorter than its diff:
```python
import functools
import jax
import jax.numpy as jnp
from jax import lax
from jax.experimental import pallas as pl
from jax.experimental.pallas import tpu as pltpu
from jax.sharding import PartitionSpec as P

LEAD, C1, C2 = 1, 0, 0
XM, PN, FM, FN = 1024, 256, 512, 256


def tile_of(size, most):
    return most if size % most == 0 else size


def route_kernel(
    ne, nr, tok_ref, cot_ref, left_ref, right_ref, part_ref, x_late, y_late,
    tok, cot, left, right, x, y,
    plane_send, up_send, down_send, cot_send, tok_recv, cot_recv, local,
):
    e = lax.axis_index("expert")
    r = lax.axis_index("replica")
    rows = tok_ref.shape[0] // ne
    group = rows * ne
    half = group // 2
    width = tok.shape[1]
    cols = cot.shape[1]
    blocks, order = right_ref.shape[0], right_ref.shape[1]

    nc = 2 if ne % 2 == 0 else 1
    nx = 2 if ne % (2 * nc) == 0 else 1
    ny = ne // (nc * nx)
    core = e % nc
    self_k = core * (nx * ny - 1)

    def target_of(k):
        dx, dy, dc = k + core, k // nx + core, k // (nx * ny)
        return ((e // (nc * nx) + dy) % ny * nx + (e // nc + dx) % nx) * nc + (core + dc) % nc

    def at_rows(start, size):
        return pl.ds(pl.multiple_of(start, rows), size)

    def tok_at(origin, k):
        return at_rows((origin * ne + k) * rows, rows)

    def place(tr, origin):
        return jnp.where(tr >= nr // 2, origin + nr - tr, tr + nr - origin) % nr

    def cot_at(tr, origin, k):
        i = place(tr, origin)
        second = k // (ne // 2)
        split = (nr - 2) * group + second * group + (i - (nr - 2)) * half + (k - second * (ne // 2)) * rows
        return at_rows(jnp.where(i < nr - 2, i * group + k * rows, split), rows)

    def own_rows(target):
        return at_rows(target * rows, rows)

    def own_cols(target):
        return pl.ds(pl.multiple_of(target * cols, cols), cols)

    def plane_copy(k):
        target = target_of(k)
        return pltpu.make_async_remote_copy(
            tok_ref.at[own_rows(target)], tok.at[tok_at(r, k)],
            plane_send, tok_recv.at[r * ne + k],
            device_id={"expert": target, "replica": r},
        )

    def relay(origin, k, up, src):
        return pltpu.make_async_remote_copy(
            src, tok.at[tok_at(origin, k)],
            up_send if up else down_send, tok_recv.at[origin * ne + k],
            device_id={"expert": e, "replica": r + 1 if up else r - 1},
        )

    def forward(origin, k, up, src):
        ahead = (r + 1 < nr) if up else (r > 0)

        @pl.when(ahead)
        def _():
            relay(origin, k, up, src).start()

    def tok_wait(origin, k):
        pltpu.make_async_remote_copy(
            tok.at[tok_at(origin, k)], tok.at[tok_at(origin, k)],
            up_send, tok_recv.at[origin * ne + k],
            device_id={"expert": e, "replica": (r + 1) % nr},
        ).wait_recv()

    def cot_copy(k, tr):
        te = target_of(k)
        return pltpu.make_async_remote_copy(
            cot_ref.at[own_rows(te), own_cols(tr)], cot.at[cot_at(tr, r, k)],
            cot_send, cot_recv.at[r * 2 + k // (ne // 2)],
            device_id={"expert": te, "replica": tr},
        )

    def cot_wait(origin, second):
        whole = cot.at[pl.ds(0, half)]
        pltpu.make_async_remote_copy(
            whole, whole, cot_send, cot_recv.at[origin * 2 + second],
            device_id={"expert": e, "replica": (r + 1) % nr},
        ).wait_recv()

    barrier = pltpu.get_barrier_semaphore()

    @pl.loop(1, ne * nr)
    def _(k):
        pl.semaphore_signal(
            barrier, inc=1,
            device_id={"expert": (e + k % ne) % ne, "replica": (r + k // ne) % nr},
        )

    own_tok = tok_ref.at[own_rows(e)]
    pltpu.make_async_copy(own_tok, tok.at[tok_at(r, self_k)], tok_recv.at[r * ne + self_k]).start()
    pltpu.make_async_copy(
        cot_ref.at[own_rows(e), own_cols(r)], cot.at[cot_at(r, r, self_k)], cot_recv.at[r * 2]
    ).start()
    load_left = pltpu.make_async_copy(left_ref, left, local.at[0])
    load_right = pltpu.make_async_copy(right_ref, right, local.at[1])
    load_left.start()
    load_right.start()
    with jax.named_scope("bar"):
        pl.semaphore_wait(barrier, ne * nr - 1)

    @pl.loop(0, ne)
    def _(k):
        @pl.when(k != self_k)
        def _():
            plane_copy(k).start()

    def send_targets(first, end):
        @pl.loop(first, end)
        def _(k):
            def send(distances):
                for distance in distances:
                    for tr in (r + distance, r - distance):
                        @pl.when((tr >= 0) & (tr < nr))
                        def _():
                            cot_copy(k, tr).start()

            @pl.when(core == 0)
            def _():
                send(range(nr - 1, 0, -1))

            @pl.when(core != 0)
            def _():
                send(range(1, nr))

    send_targets(0, LEAD)
    forward(r, self_k, True, own_tok)
    forward(r, self_k, False, own_tok)

    with jax.named_scope("plane"):
        @pl.loop(0, ne)
        def _(k):
            @pl.when(k != self_k)
            def _():
                tok_wait(r, k)
                forward(r, k, True, tok.at[tok_at(r, k)])
                forward(r, k, False, tok.at[tok_at(r, k)])

    def relay_step(distance, k):
        for origin, up in ((r - distance, True), (r + distance, False)):
            @pl.when((origin >= 0) & (origin < nr))
            def _():
                tok_wait(origin, k)
                forward(origin, k, up, tok.at[tok_at(origin, k)])

    sent = LEAD
    for distance in range(1, nr - 1):
        more = (C1, C2)[distance - 1] if distance < 3 else 0
        with jax.named_scope("relay%d" % distance):
            @pl.loop(0, ne)
            def _(k):
                relay_step(distance, k)

                if distance == 1:
                    @pl.when(k != self_k)
                    def _():
                        cot_copy(k, r).start()

                if more:
                    @pl.when(k < more)
                    def _():
                        send_targets(sent + k, sent + k + 1)
        sent += more

    send_targets(sent, ne)

    planes = [jnp.where(r >= nr // 2, r + i, r + nr - i) % nr for i in range(nr)]

    with jax.named_scope("relay%d" % (nr - 1)):
        @pl.loop(0, ne)
        def _(k):
            relay_step(nr - 1, k)

    load_left.wait()
    tok_wait(r, self_k)
    step = tile_of(width, XM)
    for i, g in enumerate(planes):
        with jax.named_scope("x%d" % i):
            @pl.loop(0, width // step)
            def _(j):
                part = pl.ds(pl.multiple_of(j * step, step), step)
                columns = pl.ds(pl.multiple_of(g * group, group), group)
                tile = lax.dot_general(
                    left[part, :], tok[columns, :], (((1,), (1,)), ((), ())),
                    preferred_element_type=jnp.float32,
                ).astype(x.dtype)
                if i < nr - 2:
                    x[part, i * group:(i + 1) * group] = tile
                else:
                    at = (i - (nr - 2)) * half
                    x[part, (nr - 2) * group + at:(nr - 2) * group + at + half] = tile[:, :half]
                    x_late[part, at:at + half] = tile[:, half:]

    load_right.wait()

    def make_y(i, out):
        for b in range(blocks):
            inside = slice(b * order, (b + 1) * order)
            out[:, inside] = jnp.dot(
                cot[i * group:(i + 1) * group, inside], right[b], preferred_element_type=jnp.float32
            ).astype(y.dtype)

    for i in range(nr - 2):
        with jax.named_scope("yw%d" % i):
            cot_wait(planes[i], 0)
            cot_wait(planes[i], 1)
        make_y(i, y.at[i * group:(i + 1) * group])

    with jax.named_scope("ywhalf"):
        cot_wait(planes[nr - 2], 0)
        cot_wait(planes[nr - 1], 0)
    make_y(nr - 2, y.at[(nr - 2) * group:(nr - 1) * group])

    with jax.named_scope("P"):
        step = tile_of(cols, PN)

        @pl.loop(0, cols // step)
        def _(j):
            part = pl.ds(pl.multiple_of(j * step, step), step)
            part_ref[:, part] = jnp.dot(x[...], y[:, part], preferred_element_type=jnp.float32)

    def send_wait(sem, data):
        pltpu.make_async_remote_copy(
            data, data, sem, tok_recv.at[0], device_id={"expert": e, "replica": (r + 1) % nr}
        ).wait_send()

    with jax.named_scope("sends"):
        send_wait(plane_send, tok.at[pl.ds(0, group - rows)])
        send_wait(cot_send, cot.at[pl.ds(0, group * nr - rows)])
        for q in range(1, nr):
            @pl.when(r + 1 == q)
            def _():
                send_wait(up_send, tok.at[pl.ds(0, q * group)])

            @pl.when(nr - r == q)
            def _():
                send_wait(down_send, tok.at[pl.ds(0, q * group)])

    with jax.named_scope("ywlate"):
        cot_wait(planes[nr - 2], 1)
        cot_wait(planes[nr - 1], 1)
    make_y(nr - 1, y_late)


def finish_kernel(part_ref, x_ref, y_ref, out_ref):
    rows, cols = out_ref.shape
    at = pl.ds(pl.multiple_of(pl.program_id(0) * rows, rows), rows)
    step = tile_of(cols, FN)
    for j in range(cols // step):
        part = slice(j * step, (j + 1) * step)
        out_ref[:, part] = (
            part_ref[at, part]
            + jnp.dot(x_ref[at, :], y_ref[:, part], preferred_element_type=jnp.float32)
        ).astype(out_ref.dtype)


def body(tokens_in, cotangents, left_root, right_root):
    ne, nr = lax.axis_size("expert"), lax.axis_size("replica")
    assert left_root.shape[0] == 1
    width = tokens_in.shape[1]
    columns = cotangents.shape[1] // nr
    total = tokens_in.shape[0] * nr
    group = tokens_in.shape[0]
    blocks, order = right_root.shape[1], right_root.shape[2]
    anywhere = pl.BlockSpec(memory_space=pl.ANY)
    vmem = pl.BlockSpec(memory_space=pltpu.VMEM)
    dtype = jnp.bfloat16
    dma = pltpu.SemaphoreType.DMA
    part, x_late, y_late = pl.pallas_call(
        functools.partial(route_kernel, ne, nr),
        out_shape=[
            pltpu.VMEM((width, columns), jnp.float32),
            pltpu.VMEM((width, group), dtype),
            pltpu.VMEM((group, columns), dtype),
        ],
        in_specs=[anywhere] * 4,
        out_specs=[vmem] * 3,
        scratch_shapes=[
            pltpu.VMEM((total, width), dtype),
            pltpu.VMEM((total, columns), dtype),
            pltpu.VMEM((width, width), dtype),
            pltpu.VMEM((blocks, order, order), dtype),
            pltpu.VMEM((width, total - group), dtype),
            pltpu.VMEM((total - group, columns), dtype),
            dma, dma, dma, dma, dma((ne * nr,)), dma((2 * nr,)), dma((2,)),
        ],
        compiler_params=pltpu.CompilerParams(
            collective_id=0, has_side_effects=True, vmem_limit_bytes=38 * 1024 * 1024
        ),
    )(tokens_in, cotangents, left_root[0], right_root[0])
    step = tile_of(width, FM)
    out = pl.pallas_call(
        finish_kernel,
        out_shape=jax.ShapeDtypeStruct((width, columns), dtype),
        grid=(width // step,),
        in_specs=[vmem] * 3,
        out_specs=pl.BlockSpec((step, columns), lambda i: (i, 0)),
        compiler_params=pltpu.CompilerParams(vmem_limit_bytes=12 * 1024 * 1024),
    )(part, x_late, y_late)
    return out[None]


def solution(mesh):
    in_specs = (
        P(("expert", "replica"), None),
        P(("expert", "replica"), None),
        P("expert", None, None),
        P("expert", "replica", None, None),
    )
    out_specs = P("expert", None, "replica")
    return jax.shard_map(body, mesh=mesh, in_specs=in_specs, out_specs=out_specs, check_vma=False)
```

time: 172 us -> 151 us (0.88)
  matrix products: 13.9 us -> 0 us
  Pallas kernels: 155 us -> 149 us
    dot_general x1 -> x0, matrix products: 13.9 us -> none  [body(): return jnp.dot(x, y, preferred_element_type=jnp.float32).astype(dtype)[None]]
    pallas_call x1 -> x2, Pallas kernels: 155 us -> 149 us  [the longest x1 144 us: body(): pl.pallas_call(functools.partial(route_kernel, ne, nr), out_shape=[pltpu....]
where the time goes in v1:
time: 151 us; the launch traced here: 149 us
  Pallas kernels  149 us (99%)
    pallas_call x1, Pallas kernels, body(): pl.pallas_call(functools.partial(route_kernel, ne, nr), out_shape=[pltpu....  144 us
    pallas_call x1, Pallas kernels, body(): pl.pallas_call(finish_kernel, out_shape=jax.ShapeDtypeStruct((width, colu...  4.82 us

profile of v1, /device:TPU:1, one launch (start us, length us, event | category | flops | bytes accessed | tf_op | source)
XLA Modules:
  0.0 148.8 jit_solution(885209294049300980)
XLA Ops:
  0.0 144.0 %shard_map.46 = (f32[2048,2048]{1,0:T(8,128)S(1)}, bf16[2048,256]{1,0:T(8,128)(2,1)S(1)}, bf16[256,2048]{1,0:T(8,128)(2,1)S(1)}) custom-call(bf16[256,2048]{1,0:T(8,128)(2,1)} %tok_ref.1, bf16[256,8192]{1,0:T(8,128)(2,1)} %cot_ref.1, bf16[2048,2048]{1,0:T(8,128)(2,1)} %bitcast.3, bf16[2,1024,1024]{2,1,0:T(8,128)(2,1)} %bitcast.4), custom_call_target="tpu_custom_call" | custom-call | tf_op jit(solution)/shard_map/pallas_call | solution.py:294
  144.0 4.8 %shard_map.47 = bf16[2048,2048]{1,0:T(8,128)(2,1)} custom-call(f32[2048,2048]{1,0:T(8,128)S(1)} %get-tuple-element.8.part_ref, bf16[2048,256]{1,0:T(8,128)(2,1)S(1)} %get-tuple-element.9.x_ref, bf16[256,2048]{1,0:T(8,128)(2,1)S(1)} %get-tuple-element.10.y_ref), custom_call_target="tpu_custom_call" | custom-call | tf_op jit(solution)/shard_map/pallas_call | solution.py:317

commit v2 on v1

--- a/solution.py
+++ b/solution.py
@@ -6,8 +6,8 @@
 from jax.experimental.pallas import tpu as pltpu
 from jax.sharding import PartitionSpec as P
 
-LEAD, C1, C2 = 1, 0, 0
-XM, PN, FM, FN = 1024, 256, 512, 256
+LEAD, C1, C2, AHEAD = 1, 0, 1, 1
+XM, PN, FM = 1024, 256, 256
 
 
 def tile_of(size, most):
@@ -15,8 +15,8 @@
 
 
 def route_kernel(
-    ne, nr, tok_ref, cot_ref, left_ref, right_ref, part_ref, x_late, y_late,
-    tok, cot, left, right, x, y,
+    ne, nr, tok_ref, cot_ref, left_ref, right_ref, x_late, cot, right, part_ref,
+    tok, left, x, y, low, high,
     plane_send, up_send, down_send, cot_send, tok_recv, cot_recv, local,
 ):
     e = lax.axis_index("expert")
@@ -104,13 +104,19 @@
         ).wait_recv()
 
     barrier = pltpu.get_barrier_semaphore()
-
-    @pl.loop(1, ne * nr)
+    above, below = r + 1 < nr, r > 0
+
+    @pl.loop(1, ne)
     def _(k):
-        pl.semaphore_signal(
-            barrier, inc=1,
-            device_id={"expert": (e + k % ne) % ne, "replica": (r + k // ne) % nr},
-        )
+        pl.semaphore_signal(barrier, inc=1, device_id={"expert": (e + k) % ne, "replica": r})
+
+    def tell(up, sem):
+        @pl.when(above if up else below)
+        def _():
+            pl.semaphore_signal(sem, inc=1, device_id={"expert": e, "replica": r + 1 if up else r - 1})
+
+    tell(True, barrier)
+    tell(False, barrier)
 
     own_tok = tok_ref.at[own_rows(e)]
     pltpu.make_async_copy(own_tok, tok.at[tok_at(r, self_k)], tok_recv.at[r * ne + self_k]).start()
@@ -122,7 +128,9 @@
     load_left.start()
     load_right.start()
     with jax.named_scope("bar"):
-        pl.semaphore_wait(barrier, ne * nr - 1)
+        pl.semaphore_wait(barrier, ne - 1 + above.astype(jnp.int32) + below.astype(jnp.int32))
+    tell(True, low.at[0])
+    tell(False, high.at[0])
 
     @pl.loop(0, ne)
     def _(k):
@@ -130,15 +138,25 @@
         def _():
             plane_copy(k).start()
 
+    def send_cots(k, distance):
+        for tr in (r + distance, r - distance):
+            @pl.when((tr >= 0) & (tr < nr))
+            def _():
+                cot_copy(k, tr).start()
+
+    steps = ne + AHEAD * (nr - 2)
+
     def send_targets(first, end):
         @pl.loop(first, end)
-        def _(k):
+        def _(step):
             def send(distances):
                 for distance in distances:
-                    for tr in (r + distance, r - distance):
-                        @pl.when((tr >= 0) & (tr < nr))
-                        def _():
-                            cot_copy(k, tr).start()
+                    k = step - AHEAD * (nr - 1 - distance)
+                    ok = (k >= 0) & (k < ne)
+
+                    @pl.when(ok & (k != self_k) if distance == 1 else ok)
+                    def _():
+                        send_cots(k, distance)
 
             @pl.when(core == 0)
             def _():
@@ -148,9 +166,25 @@
             def _():
                 send(range(1, nr))
 
-    send_targets(0, LEAD)
     forward(r, self_k, True, own_tok)
     forward(r, self_k, False, own_tok)
+    send_cots(self_k, 1)
+
+    with jax.named_scope("ready"):
+        for distance in range(1, nr):
+            @pl.when(r >= distance)
+            def _():
+                pl.semaphore_wait(low.at[distance - 1], 1)
+                if distance + 1 < nr:
+                    tell(True, low.at[distance])
+
+            @pl.when(r + distance < nr)
+            def _():
+                pl.semaphore_wait(high.at[distance - 1], 1)
+                if distance + 1 < nr:
+                    tell(False, high.at[distance])
+
+    send_targets(0, LEAD)
 
     with jax.named_scope("plane"):
         @pl.loop(0, ne)
@@ -187,7 +221,7 @@
                         send_targets(sent + k, sent + k + 1)
         sent += more
 
-    send_targets(sent, ne)
+    send_targets(sent, steps)
 
     planes = [jnp.where(r >= nr // 2, r + i, r + nr - i) % nr for i in range(nr)]
 
@@ -264,19 +298,30 @@
     with jax.named_scope("ywlate"):
         cot_wait(planes[nr - 2], 1)
         cot_wait(planes[nr - 1], 1)
-    make_y(nr - 1, y_late)
-
-
-def finish_kernel(part_ref, x_ref, y_ref, out_ref):
-    rows, cols = out_ref.shape
-    at = pl.ds(pl.multiple_of(pl.program_id(0) * rows, rows), rows)
-    step = tile_of(cols, FN)
-    for j in range(cols // step):
-        part = slice(j * step, (j + 1) * step)
-        out_ref[:, part] = (
-            part_ref[at, part]
-            + jnp.dot(x_ref[at, :], y_ref[:, part], preferred_element_type=jnp.float32)
-        ).astype(out_ref.dtype)
+
+
+def finish_kernel(x_ref, cot_ref, right_ref, part_ref, out_ref, y, out, sem):
+    width, group = x_ref.shape
+    total, order = cot_ref.shape[0], right_ref.shape[1]
+    step = tile_of(width, FM)
+    stores = []
+    for b in range(right_ref.shape[0]):
+        inside = slice(b * order, (b + 1) * order)
+        y[:, inside] = jnp.dot(
+            cot_ref[total - group:, inside], right_ref[b], preferred_element_type=jnp.float32
+        ).astype(y.dtype)
+        for i in range(width // step):
+            part = slice(i * step, (i + 1) * step)
+            out[part, inside] = (
+                part_ref[part, inside]
+                + jnp.dot(x_ref[part, :], y[:, inside], preferred_element_type=jnp.float32)
+            ).astype(out.dtype)
+            stores.append(
+                pltpu.make_async_copy(out.at[part, inside], out_ref.at[part, inside], sem.at[len(stores)])
+            )
+            stores[-1].start()
+    for store in stores:
+        store.wait()
 
 
 def body(tokens_in, cotangents, left_root, right_root):
@@ -291,37 +336,40 @@
     vmem = pl.BlockSpec(memory_space=pltpu.VMEM)
     dtype = jnp.bfloat16
     dma = pltpu.SemaphoreType.DMA
-    part, x_late, y_late = pl.pallas_call(
+    regular = pltpu.SemaphoreType.REGULAR
+    kept = pl.pallas_call(
         functools.partial(route_kernel, ne, nr),
         out_shape=[
+            pltpu.VMEM((width, group), dtype),
+            pltpu.VMEM((total, columns), dtype),
+            pltpu.VMEM((blocks, order, order), dtype),
             pltpu.VMEM((width, columns), jnp.float32),
-            pltpu.VMEM((width, group), dtype),
-            pltpu.VMEM((group, columns), dtype),
         ],
         in_specs=[anywhere] * 4,
-        out_specs=[vmem] * 3,
+        out_specs=[vmem] * 4,
         scratch_shapes=[
             pltpu.VMEM((total, width), dtype),
-            pltpu.VMEM((total, columns), dtype),
             pltpu.VMEM((width, width), dtype),
-            pltpu.VMEM((blocks, order, order), dtype),
             pltpu.VMEM((width, total - group), dtype),
             pltpu.VMEM((total - group, columns), dtype),
+            regular((nr - 1,)), regular((nr - 1,)),
             dma, dma, dma, dma, dma((ne * nr,)), dma((2 * nr,)), dma((2,)),
         ],
         compiler_params=pltpu.CompilerParams(
-            collective_id=0, has_side_effects=True, vmem_limit_bytes=38 * 1024 * 1024
+            collective_id=0, has_side_effects=True, vmem_limit_bytes=34 * 1024 * 1024
         ),
     )(tokens_in, cotangents, left_root[0], right_root[0])
-    step = tile_of(width, FM)
     out = pl.pallas_call(
         finish_kernel,
         out_shape=jax.ShapeDtypeStruct((width, columns), dtype),
-        grid=(width // step,),
-        in_specs=[vmem] * 3,
-        out_specs=pl.BlockSpec((step, columns), lambda i: (i, 0)),
-        compiler_params=pltpu.CompilerParams(vmem_limit_bytes=12 * 1024 * 1024),
-    )(part, x_late, y_late)
+        in_specs=[vmem] * 4,
+        out_specs=anywhere,
+        scratch_shapes=[
+            pltpu.VMEM((group, columns), dtype), pltpu.VMEM((width, columns), dtype),
+            dma((blocks * (width // tile_of(width, FM)),)),
+        ],
+        compiler_params=pltpu.CompilerParams(vmem_limit_bytes=16 * 1024 * 1024),
+    )(*kept)
     return out[None]
 
 

time: 151 us -> 147 us (0.974); the launches traced: 149 us -> 146 us
  Pallas kernels: 149 us -> 146 us
    pallas_call x1, Pallas kernels: 144 us -> 142 us  [body(): pl.pallas_call(functools.partial(route_kernel, ne, nr), out_shape=[pltpu....]
where the time goes in v2:
time: 147 us; the launch traced here: 146 us
  Pallas kernels  146 us (99%)
    pallas_call x1, Pallas kernels, body(): pl.pallas_call(functools.partial(route_kernel, ne, nr), out_shape=[pltpu....  142 us
    pallas_call x1, Pallas kernels, body(): pl.pallas_call(finish_kernel, out_shape=jax.ShapeDtypeStruct((width, colu...  4.67 us

profile of v2, /device:TPU:1, one launch (start us, length us, event | category | flops | bytes accessed | tf_op | source)
XLA Modules:
  0.0 146.5 jit_solution(15079122872329595853)
XLA Ops:
  0.0 141.8 %shard_map.46 = (bf16[2048,256]{1,0:T(8,128)(2,1)S(1)}, bf16[1024,2048]{1,0:T(8,128)(2,1)S(1)}, bf16[2,1024,1024]{2,1,0:T(8,128)(2,1)S(1)}, f32[2048,2048]{1,0:T(8,128)S(1)}) custom-call(bf16[256,2048]{1,0:T(8,128)(2,1)} %tok_ref.1, bf16[256,8192]{1,0:T(8,128)(2,1)} %cot_ref.1, bf16[2048,2048]{1,0:T(8,128)(2,1)} %bitcast.3, bf16[2,1024,1024]{2,1,0:T(8,128)(2,1)} %bitcast.4), custom_call_target="tpu_custom_call" | custom-call | tf_op jit(solution)/shard_map/pallas_call | solution.py:340
  141.8 4.7 %shard_map.47 = bf16[2048,2048]{1,0:T(8,128)(2,1)} custom-call(bf16[2048,256]{1,0:T(8,128)(2,1)S(1)} %get-tuple-element.9.x_ref, bf16[1024,2048]{1,0:T(8,128)(2,1)S(1)} %get-tuple-element.10.cot_ref, bf16[2,1024,1024]{2,1,0:T(8,128)(2,1)S(1)} %get-tuple-element.11.right_ref, f32[2048,2048]{1,0:T(8,128)S(1)} %get-tuple-element.12.part_ref), custom_call_target="tpu_custom_call" | custom-call | tf_op jit(solution)/shard_map/pallas_call | solution.py:362

commit v3 on v2

--- a/solution.py
+++ b/solution.py
@@ -15,7 +15,7 @@
 
 
 def route_kernel(
-    ne, nr, tok_ref, cot_ref, left_ref, right_ref, x_late, cot, right, part_ref,
+    ne, nr, tok_ref, cot_ref, left_ref, right_ref, x_late, cot, right, done, part_ref,
     tok, left, x, y, low, high,
     plane_send, up_send, down_send, cot_send, tok_recv, cot_recv, local,
 ):
@@ -88,20 +88,46 @@
             device_id={"expert": e, "replica": (r + 1) % nr},
         ).wait_recv()
 
-    def cot_copy(k, tr):
+    first = cols - order
+    whole_piece, first_blocks, last_block = (0, cols), (0, first), (first, order)
+
+    def cot_copy(k, tr, columns, sem):
         te = target_of(k)
+        start, size = columns
         return pltpu.make_async_remote_copy(
-            cot_ref.at[own_rows(te), own_cols(tr)], cot.at[cot_at(tr, r, k)],
-            cot_send, cot_recv.at[r * 2 + k // (ne // 2)],
+            cot_ref.at[own_rows(te), pl.ds(pl.multiple_of(tr * cols + start, order), size)],
+            cot.at[cot_at(tr, r, k), pl.ds(start, size)],
+            cot_send, cot_recv.at[r * 3 + sem],
             device_id={"expert": te, "replica": tr},
         )
 
-    def cot_wait(origin, second):
-        whole = cot.at[pl.ds(0, half)]
-        pltpu.make_async_remote_copy(
-            whole, whole, cot_send, cot_recv.at[origin * 2 + second],
-            device_id={"expert": e, "replica": (r + 1) % nr},
-        ).wait_recv()
+    def send_piece(k, tr):
+        @pl.when(k < ne // 2)
+        def _():
+            cot_copy(k, tr, whole_piece, 0).start()
+
+        @pl.when(k >= ne // 2)
+        def _():
+            if first:
+                cot_copy(k, tr, first_blocks, 1).start()
+
+            @pl.when(place(tr, r) < nr - 2)
+            def _():
+                cot_copy(k, tr, last_block, 2).start()
+
+    def send_last_block(k, tr):
+        @pl.when(place(tr, r) >= nr - 2)
+        def _():
+            cot_copy(k, tr, last_block, 2).start()
+
+    def cot_wait(origin, sem):
+        start, size = (whole_piece, first_blocks, last_block)[sem]
+        if size:
+            piece = cot.at[pl.ds(0, half), pl.ds(start, size)]
+            pltpu.make_async_remote_copy(
+                piece, piece, cot_send, cot_recv.at[origin * 3 + sem],
+                device_id={"expert": e, "replica": (r + 1) % nr},
+            ).wait_recv()
 
     barrier = pltpu.get_barrier_semaphore()
     above, below = r + 1 < nr, r > 0
@@ -121,7 +147,7 @@
     own_tok = tok_ref.at[own_rows(e)]
     pltpu.make_async_copy(own_tok, tok.at[tok_at(r, self_k)], tok_recv.at[r * ne + self_k]).start()
     pltpu.make_async_copy(
-        cot_ref.at[own_rows(e), own_cols(r)], cot.at[cot_at(r, r, self_k)], cot_recv.at[r * 2]
+        cot_ref.at[own_rows(e), own_cols(r)], cot.at[cot_at(r, r, self_k)], cot_recv.at[r * 3]
     ).start()
     load_left = pltpu.make_async_copy(left_ref, left, local.at[0])
     load_right = pltpu.make_async_copy(right_ref, right, local.at[1])
@@ -138,33 +164,33 @@
         def _():
             plane_copy(k).start()
 
-    def send_cots(k, distance):
+    def send_cots(k, distance, send=send_piece):
         for tr in (r + distance, r - distance):
             @pl.when((tr >= 0) & (tr < nr))
             def _():
-                cot_copy(k, tr).start()
-
-    steps = ne + AHEAD * (nr - 2)
-
-    def send_targets(first, end):
-        @pl.loop(first, end)
+                send(k, tr)
+
+    lag = AHEAD * (nr - 2)
+
+    def send_targets(begin, end, send=send_piece, k0=0):
+        @pl.loop(begin, end)
         def _(step):
-            def send(distances):
+            def send_all(distances):
                 for distance in distances:
-                    k = step - AHEAD * (nr - 1 - distance)
-                    ok = (k >= 0) & (k < ne)
+                    k = k0 + step - AHEAD * (nr - 1 - distance)
+                    ok = (k >= k0) & (k < ne)
 
                     @pl.when(ok & (k != self_k) if distance == 1 else ok)
                     def _():
-                        send_cots(k, distance)
+                        send_cots(k, distance, send)
 
             @pl.when(core == 0)
             def _():
-                send(range(nr - 1, 0, -1))
+                send_all(range(nr - 1, 0, -1))
 
             @pl.when(core != 0)
             def _():
-                send(range(1, nr))
+                send_all(range(1, nr))
 
     forward(r, self_k, True, own_tok)
     forward(r, self_k, False, own_tok)
@@ -213,7 +239,7 @@
                 if distance == 1:
                     @pl.when(k != self_k)
                     def _():
-                        cot_copy(k, r).start()
+                        send_piece(k, r)
 
                 if more:
                     @pl.when(k < more)
@@ -221,7 +247,8 @@
                         send_targets(sent + k, sent + k + 1)
         sent += more
 
-    send_targets(sent, steps)
+    send_targets(sent, ne + lag)
+    send_targets(0, ne // 2 + lag, send_last_block, ne // 2)
 
     planes = [jnp.where(r >= nr // 2, r + i, r + nr - i) % nr for i in range(nr)]
 
@@ -252,36 +279,54 @@
 
     load_right.wait()
 
-    def make_y(i, out):
-        for b in range(blocks):
+    def make_y(begin, blocks_of):
+        for b in blocks_of:
             inside = slice(b * order, (b + 1) * order)
-            out[:, inside] = jnp.dot(
-                cot[i * group:(i + 1) * group, inside], right[b], preferred_element_type=jnp.float32
+            y[begin:begin + group, inside] = jnp.dot(
+                cot[begin:begin + group, inside], right[b], preferred_element_type=jnp.float32
             ).astype(y.dtype)
 
+    early = (nr - 1) * group
     for i in range(nr - 2):
         with jax.named_scope("yw%d" % i):
-            cot_wait(planes[i], 0)
-            cot_wait(planes[i], 1)
-        make_y(i, y.at[i * group:(i + 1) * group])
+            for sem in range(3):
+                cot_wait(planes[i], sem)
+        make_y(i * group, range(blocks))
 
     with jax.named_scope("ywhalf"):
         cot_wait(planes[nr - 2], 0)
         cot_wait(planes[nr - 1], 0)
-    make_y(nr - 2, y.at[(nr - 2) * group:(nr - 1) * group])
+    make_y(early - group, range(blocks))
 
     with jax.named_scope("P"):
-        step = tile_of(cols, PN)
-
-        @pl.loop(0, cols // step)
+        step = tile_of(order, PN)
+
+        @pl.loop(0, order // step)
         def _(j):
-            part = pl.ds(pl.multiple_of(j * step, step), step)
-            part_ref[:, part] = jnp.dot(x[...], y[:, part], preferred_element_type=jnp.float32)
+            at = pl.multiple_of(j * step, step)
+            part_ref[:, pl.ds(at, step)] = jnp.dot(
+                x[...], y[:early, pl.ds(first + at, step)], preferred_element_type=jnp.float32
+            )
 
     def send_wait(sem, data):
         pltpu.make_async_remote_copy(
             data, data, sem, tok_recv.at[0], device_id={"expert": e, "replica": (r + 1) % nr}
         ).wait_send()
+
+    if first:
+        with jax.named_scope("ywfirst"):
+            cot_wait(planes[nr - 2], 1)
+            cot_wait(planes[nr - 1], 1)
+        make_y(early, range(blocks - 1))
+
+        with jax.named_scope("done"):
+            @pl.loop(0, first // step)
+            def _(j):
+                at = pl.ds(pl.multiple_of(j * step, step), step)
+                done[:, at] = (
+                    jnp.dot(x[...], y[:early, at], preferred_element_type=jnp.float32)
+                    + jnp.dot(x_late[...], y[early:, at], preferred_element_type=jnp.float32)
+                ).astype(done.dtype)
 
     with jax.named_scope("sends"):
         send_wait(plane_send, tok.at[pl.ds(0, group - rows)])
@@ -296,32 +341,37 @@
                 send_wait(down_send, tok.at[pl.ds(0, q * group)])
 
     with jax.named_scope("ywlate"):
-        cot_wait(planes[nr - 2], 1)
-        cot_wait(planes[nr - 1], 1)
-
-
-def finish_kernel(x_ref, cot_ref, right_ref, part_ref, out_ref, y, out, sem):
+        cot_wait(planes[nr - 2], 2)
+        cot_wait(planes[nr - 1], 2)
+
+
+def finish_kernel(x_ref, cot_ref, right_ref, done_ref, part_ref, out_ref, y, out, sem):
     width, group = x_ref.shape
     total, order = cot_ref.shape[0], right_ref.shape[1]
+    blocks = right_ref.shape[0]
+    first = (blocks - 1) * order
+    inside = slice(first, first + order)
     step = tile_of(width, FM)
     stores = []
-    for b in range(right_ref.shape[0]):
-        inside = slice(b * order, (b + 1) * order)
-        y[:, inside] = jnp.dot(
-            cot_ref[total - group:, inside], right_ref[b], preferred_element_type=jnp.float32
-        ).astype(y.dtype)
-        for i in range(width // step):
-            part = slice(i * step, (i + 1) * step)
-            out[part, inside] = (
-                part_ref[part, inside]
-                + jnp.dot(x_ref[part, :], y[:, inside], preferred_element_type=jnp.float32)
-            ).astype(out.dtype)
-            stores.append(
-                pltpu.make_async_copy(out.at[part, inside], out_ref.at[part, inside], sem.at[len(stores)])
-            )
-            stores[-1].start()
-    for store in stores:
-        store.wait()
+
+    def store(data, at, columns):
+        stores.append(pltpu.make_async_copy(data, out_ref.at[at, columns], sem.at[len(stores)]))
+        stores[-1].start()
+
+    tiles = [slice(i * step, (i + 1) * step) for i in range(width // step)]
+    if first:
+        for at in tiles:
+            store(done_ref.at[at], at, slice(0, first))
+    y[...] = jnp.dot(
+        cot_ref[total - group:, inside], right_ref[blocks - 1], preferred_element_type=jnp.float32
+    ).astype(y.dtype)
+    for at in tiles:
+        out[at, :] = (
+            part_ref[at, :] + jnp.dot(x_ref[at, :], y[...], preferred_element_type=jnp.float32)
+        ).astype(out.dtype)
+        store(out.at[at], at, inside)
+    for copy in stores:
+        copy.wait()
 
 
 def body(tokens_in, cotangents, left_root, right_root):
@@ -343,17 +393,18 @@
             pltpu.VMEM((width, group), dtype),
             pltpu.VMEM((total, columns), dtype),
             pltpu.VMEM((blocks, order, order), dtype),
-            pltpu.VMEM((width, columns), jnp.float32),
+            pltpu.VMEM((width, max(columns - order, 128)), dtype),
+            pltpu.VMEM((width, order), jnp.float32),
         ],
         in_specs=[anywhere] * 4,
-        out_specs=[vmem] * 4,
+        out_specs=[vmem] * 5,
         scratch_shapes=[
             pltpu.VMEM((total, width), dtype),
             pltpu.VMEM((width, width), dtype),
             pltpu.VMEM((width, total - group), dtype),
-            pltpu.VMEM((total - group, columns), dtype),
+            pltpu.VMEM((total, columns), dtype),
             regular((nr - 1,)), regular((nr - 1,)),
-            dma, dma, dma, dma, dma((ne * nr,)), dma((2 * nr,)), dma((2,)),
+            dma, dma, dma, dma, dma((ne * nr,)), dma((3 * nr,)), dma((2,)),
         ],
         compiler_params=pltpu.CompilerParams(
             collective_id=0, has_side_effects=True, vmem_limit_bytes=34 * 1024 * 1024
@@ -362,11 +413,11 @@
     out = pl.pallas_call(
         finish_kernel,
         out_shape=jax.ShapeDtypeStruct((width, columns), dtype),
-        in_specs=[vmem] * 4,
+        in_specs=[vmem] * 5,
         out_specs=anywhere,
         scratch_shapes=[
-            pltpu.VMEM((group, columns), dtype), pltpu.VMEM((width, columns), dtype),
-            dma((blocks * (width // tile_of(width, FM)),)),
+            pltpu.VMEM((group, order), dtype), pltpu.VMEM((width, order), dtype),
+            dma((2 * (width // tile_of(width, FM)),)),
         ],
         compiler_params=pltpu.CompilerParams(vmem_limit_bytes=16 * 1024 * 1024),
     )(*kept)

time: 147 us -> 145 us (0.986)
  no operation moved by 1% of the time
where the time goes in v3:
time: 145 us
  Pallas kernels  145 us (100%)
    pallas_call x1, Pallas kernels, body(): pl.pallas_call(functools.partial(route_kernel, ne, nr), out_shape=[pltpu....  142 us
    pallas_call x1, Pallas kernels, body(): pl.pallas_call(finish_kernel, out_shape=jax.ShapeDtypeStruct((width, colu...  3.45 us

profile of v3, /device:TPU:1, one launch (start us, length us, event | category | flops | bytes accessed | tf_op | source)
XLA Modules:
  0.0 145.3 jit_solution(16895466218628009307)
XLA Ops:
  0.0 141.8 %shard_map.46 = (bf16[2048,256]{1,0:T(8,128)(2,1)S(1)}, bf16[1024,2048]{1,0:T(8,128)(2,1)S(1)}, bf16[2,1024,1024]{2,1,0:T(8,128)(2,1)S(1)}, bf16[2048,1024]{1,0:T(8,128)(2,1)S(1)}, f32[2048,1024]{1,0:T(8,128)S(1)}) custom-call(bf16[256,2048]{1,0:T(8,128)(2,1)} %tok_ref.1, bf16[256,8192]{1,0:T(8,128)(2,1)} %cot_ref.1, bf16[2048,2048]{1,0:T(8,128)(2,1)} %bitcast.3, ...), custom_call_target="tpu_custom_call" | custom-call | tf_op jit(solution)/shard_map/pallas_call | solution.py:390
  141.8 3.4 %shard_map.47 = bf16[2048,2048]{1,0:T(8,128)(2,1)} custom-call(bf16[2048,256]{1,0:T(8,128)(2,1)S(1)} %get-tuple-element.10.x_ref, bf16[1024,2048]{1,0:T(8,128)(2,1)S(1)} %get-tuple-element.11.cot_ref, bf16[2,1024,1024]{2,1,0:T(8,128)(2,1)S(1)} %get-tuple-element.12.right_ref, bf16[2048,1024]{1,0:T(8,128)(2,1)S(1)} %get-tuple-element.13.done_ref, ...), custom_call_target="tpu_custom_call" | custom-call | tf_op jit(solution)/shard_map/pallas_call | solution.py:413

commit v4 on v3

--- a/solution.py
+++ b/solution.py
@@ -6,7 +6,7 @@
 from jax.experimental.pallas import tpu as pltpu
 from jax.sharding import PartitionSpec as P
 
-LEAD, C1, C2, AHEAD = 1, 0, 1, 1
+LEAD, C1, C2, AHEAD, PRE = 1, 0, 1, 1, (1,)
 XM, PN, FM = 1024, 256, 256
 
 
@@ -14,9 +14,20 @@
     return most if size % most == 0 else size
 
 
+def plane_of(ne):
+    nc = 2 if ne % 2 == 0 else 1
+    nx = 2 if ne % (2 * nc) == 0 else 1
+    return nc, nx, ne // (nc * nx)
+
+
+def rounds_of(ne):
+    nc, nx, ny = plane_of(ne)
+    return max((nc > 1) + (nx > 1) + ny // 2 - 1, 1)
+
+
 def route_kernel(
     ne, nr, tok_ref, cot_ref, left_ref, right_ref, x_late, cot, right, done, part_ref,
-    tok, left, x, y, low, high,
+    tok, left, x, y, word, low, high,
     plane_send, up_send, down_send, cot_send, tok_recv, cot_recv, local,
 ):
     e = lax.axis_index("expert")
@@ -28,15 +39,15 @@
     cols = cot.shape[1]
     blocks, order = right_ref.shape[0], right_ref.shape[1]
 
-    nc = 2 if ne % 2 == 0 else 1
-    nx = 2 if ne % (2 * nc) == 0 else 1
-    ny = ne // (nc * nx)
+    nc, nx, ny = plane_of(ne)
     core = e % nc
     self_k = core * (nx * ny - 1)
 
+    def expert_at(dc, dx, dy):
+        return ((e // (nc * nx) + dy) % ny * nx + (e // nc + dx) % nx) * nc + (e + dc) % nc
+
     def target_of(k):
-        dx, dy, dc = k + core, k // nx + core, k // (nx * ny)
-        return ((e // (nc * nx) + dy) % ny * nx + (e // nc + dx) % nx) * nc + (core + dc) % nc
+        return expert_at(k // (nx * ny), k + core, k // nx + core)
 
     def at_rows(start, size):
         return pl.ds(pl.multiple_of(start, rows), size)
@@ -132,9 +143,14 @@
     barrier = pltpu.get_barrier_semaphore()
     above, below = r + 1 < nr, r > 0
 
-    @pl.loop(1, ne)
-    def _(k):
-        pl.semaphore_signal(barrier, inc=1, device_id={"expert": (e + k) % ne, "replica": r})
+    sides = [(1, 0, 0)] * (nc > 1) + [(0, 1, 0)] * (nx > 1) + [(0, 0, dy) for dy in sorted({1, ny - 1} - {0})]
+    rounds = word.shape[0]
+
+    def tell_sides(sem):
+        for side in sides:
+            pl.semaphore_signal(sem, inc=1, device_id={"expert": expert_at(*side), "replica": r})
+
+    tell_sides(barrier)
 
     def tell(up, sem):
         @pl.when(above if up else below)
@@ -154,15 +170,7 @@
     load_left.start()
     load_right.start()
     with jax.named_scope("bar"):
-        pl.semaphore_wait(barrier, ne - 1 + above.astype(jnp.int32) + below.astype(jnp.int32))
-    tell(True, low.at[0])
-    tell(False, high.at[0])
-
-    @pl.loop(0, ne)
-    def _(k):
-        @pl.when(k != self_k)
-        def _():
-            plane_copy(k).start()
+        pl.semaphore_wait(barrier, len(sides) + above.astype(jnp.int32) + below.astype(jnp.int32))
 
     def send_cots(k, distance, send=send_piece):
         for tr in (r + distance, r - distance):
@@ -171,16 +179,23 @@
                 send(k, tr)
 
     lag = AHEAD * (nr - 2)
-
-    def send_targets(begin, end, send=send_piece, k0=0):
+    pre = PRE
+
+    def send_targets(begin, end, send=send_piece, k0=0, order_of=lambda k: k):
         @pl.loop(begin, end)
         def _(step):
             def send_all(distances):
                 for distance in distances:
-                    k = k0 + step - AHEAD * (nr - 1 - distance)
-                    ok = (k >= k0) & (k < ne)
-
-                    @pl.when(ok & (k != self_k) if distance == 1 else ok)
+                    k = step - AHEAD * (nr - 1 - distance)
+                    ok = (k >= 0) & (k < ne - k0)
+                    k = order_of(k) + k0
+
+                    if distance == 1:
+                        ok &= k != self_k
+                        for sent_k in pre if k0 == 0 else ():
+                            ok &= k != sent_k
+
+                    @pl.when(ok)
                     def _():
                         send_cots(k, distance, send)
 
@@ -196,6 +211,19 @@
     forward(r, self_k, False, own_tok)
     send_cots(self_k, 1)
 
+    with jax.named_scope("rounds"):
+        for t in range(rounds):
+            tell_sides(word.at[t])
+            pl.semaphore_wait(word.at[t], len(sides))
+        tell(True, low.at[0])
+        tell(False, high.at[0])
+
+    @pl.loop(0, ne)
+    def _(k):
+        @pl.when(k != self_k)
+        def _():
+            plane_copy(k).start()
+
     with jax.named_scope("ready"):
         for distance in range(1, nr):
             @pl.when(r >= distance)
@@ -209,6 +237,10 @@
                 pl.semaphore_wait(high.at[distance - 1], 1)
                 if distance + 1 < nr:
                     tell(False, high.at[distance])
+
+            if distance == 1:
+                for k in pre:
+                    send_cots(k, 1)
 
     send_targets(0, LEAD)
 
@@ -227,6 +259,10 @@
             def _():
                 tok_wait(origin, k)
                 forward(origin, k, up, tok.at[tok_at(origin, k)])
+
+    def own_column_last(k):
+        turned = jnp.where(k < ne // 4, k + ne // 4, ne // 2 - 1 - k)
+        return jnp.where(core == 0, turned, k)
 
     sent = LEAD
     for distance in range(1, nr - 1):
@@ -248,7 +284,7 @@
         sent += more
 
     send_targets(sent, ne + lag)
-    send_targets(0, ne // 2 + lag, send_last_block, ne // 2)
+    send_targets(0, ne // 2 + lag, send_last_block, ne // 2, own_column_last)
 
     planes = [jnp.where(r >= nr // 2, r + i, r + nr - i) % nr for i in range(nr)]
 
@@ -403,7 +439,7 @@
             pltpu.VMEM((width, width), dtype),
             pltpu.VMEM((width, total - group), dtype),
             pltpu.VMEM((total, columns), dtype),
-            regular((nr - 1,)), regular((nr - 1,)),
+            regular((rounds_of(ne),)), regular((nr - 1,)), regular((nr - 1,)),
             dma, dma, dma, dma, dma((ne * nr,)), dma((3 * nr,)), dma((2,)),
         ],
         compiler_params=pltpu.CompilerParams(

time: 145 us -> 144 us (level)
  no operation moved by 1% of the time
where the time goes in v4:
time: 144 us
  Pallas kernels  144 us (100%)
    pallas_call x1, Pallas kernels, body(): pl.pallas_call(functools.partial(route_kernel, ne, nr), out_shape=[pltpu....  141 us
    pallas_call x1, Pallas kernels, body(): pl.pallas_call(finish_kernel, out_shape=jax.ShapeDtypeStruct((width, colu...  3.45 us

profile of v4, /device:TPU:1, one launch (start us, length us, event | category | flops | bytes accessed | tf_op | source)
XLA Modules:
  0.0 144.3 jit_solution(3613463168405217849)
XLA Ops:
  0.0 140.8 %shard_map.46 = (bf16[2048,256]{1,0:T(8,128)(2,1)S(1)}, bf16[1024,2048]{1,0:T(8,128)(2,1)S(1)}, bf16[2,1024,1024]{2,1,0:T(8,128)(2,1)S(1)}, bf16[2048,1024]{1,0:T(8,128)(2,1)S(1)}, f32[2048,1024]{1,0:T(8,128)S(1)}) custom-call(bf16[256,2048]{1,0:T(8,128)(2,1)} %tok_ref.1, bf16[256,8192]{1,0:T(8,128)(2,1)} %cot_ref.1, bf16[2048,2048]{1,0:T(8,128)(2,1)} %bitcast.3, ...), custom_call_target="tpu_custom_call" | custom-call | tf_op jit(solution)/shard_map/pallas_call | solution.py:426
  140.8 3.4 %shard_map.47 = bf16[2048,2048]{1,0:T(8,128)(2,1)} custom-call(bf16[2048,256]{1,0:T(8,128)(2,1)S(1)} %get-tuple-element.10.x_ref, bf16[1024,2048]{1,0:T(8,128)(2,1)S(1)} %get-tuple-element.11.cot_ref, bf16[2,1024,1024]{2,1,0:T(8,128)(2,1)S(1)} %get-tuple-element.12.right_ref, bf16[2048,1024]{1,0:T(8,128)(2,1)S(1)} %get-tuple-element.13.done_ref, ...), custom_call_target="tpu_custom_call" | custom-call | tf_op jit(solution)/shard_map/pallas_call | solution.py:449

commit v5 on v4

--- a/solution.py
+++ b/solution.py
@@ -6,7 +6,7 @@
 from jax.experimental.pallas import tpu as pltpu
 from jax.sharding import PartitionSpec as P
 
-LEAD, C1, C2, AHEAD, PRE = 1, 0, 1, 1, (1,)
+LEAD, C1, C2, AHEAD, PRE = 2, 0, 2, 1, (1,)
 XM, PN, FM = 1024, 256, 256
 
 
@@ -261,6 +261,7 @@
                 forward(origin, k, up, tok.at[tok_at(origin, k)])
 
     def own_column_last(k):
+        k = jnp.where(e // nc == 0, (k + ne // 2 - 1) % (ne // 2), k)
         turned = jnp.where(k < ne // 4, k + ne // 4, ne // 2 - 1 - k)
         return jnp.where(core == 0, turned, k)
 

time: 144 us -> 144 us (level)
  no operation moved by 1% of the time
where the time goes in v5:
time: 144 us
  Pallas kernels  144 us (100%)
    pallas_call x1, Pallas kernels, body(): pl.pallas_call(functools.partial(route_kernel, ne, nr), out_shape=[pltpu....  140 us
    pallas_call x1, Pallas kernels, body(): pl.pallas_call(finish_kernel, out_shape=jax.ShapeDtypeStruct((width, colu...  3.45 us

profile of v5, /device:TPU:1, one launch (start us, length us, event | category | flops | bytes accessed | tf_op | source)
XLA Modules:
  0.0 143.8 jit_solution(15120662442823094954)
XLA Ops:
  0.0 140.3 %shard_map.46 = (bf16[2048,256]{1,0:T(8,128)(2,1)S(1)}, bf16[1024,2048]{1,0:T(8,128)(2,1)S(1)}, bf16[2,1024,1024]{2,1,0:T(8,128)(2,1)S(1)}, bf16[2048,1024]{1,0:T(8,128)(2,1)S(1)}, f32[2048,1024]{1,0:T(8,128)S(1)}) custom-call(bf16[256,2048]{1,0:T(8,128)(2,1)} %tok_ref.1, bf16[256,8192]{1,0:T(8,128)(2,1)} %cot_ref.1, bf16[2048,2048]{1,0:T(8,128)(2,1)} %bitcast.3, ...), custom_call_target="tpu_custom_call" | custom-call | tf_op jit(solution)/shard_map/pallas_call | solution.py:427
  140.3 3.4 %shard_map.47 = bf16[2048,2048]{1,0:T(8,128)(2,1)} custom-call(bf16[2048,256]{1,0:T(8,128)(2,1)S(1)} %get-tuple-element.10.x_ref, bf16[1024,2048]{1,0:T(8,128)(2,1)S(1)} %get-tuple-element.11.cot_ref, bf16[2,1024,1024]{2,1,0:T(8,128)(2,1)S(1)} %get-tuple-element.12.right_ref, bf16[2048,1024]{1,0:T(8,128)(2,1)S(1)} %get-tuple-element.13.done_ref, ...), custom_call_target="tpu_custom_call" | custom-call | tf_op jit(solution)/shard_map/pallas_call | solution.py:450

commit v6 on v5

--- a/solution.py
+++ b/solution.py
@@ -6,7 +6,7 @@
 from jax.experimental.pallas import tpu as pltpu
 from jax.sharding import PartitionSpec as P
 
-LEAD, C1, C2, AHEAD, PRE = 2, 0, 2, 1, (1,)
+LEAD, C1, C2, AHEAD, PRE = 2, 0, 3, 1, (1,)
 XM, PN, FM = 1024, 256, 256
 
 

time: 144 us -> 144 us (level)
  no operation moved by 1% of the time
where the time goes in v6:
time: 144 us
  Pallas kernels  144 us (100%)
    pallas_call x1, Pallas kernels, body(): pl.pallas_call(functools.partial(route_kernel, ne, nr), out_shape=[pltpu....  140 us
    pallas_call x1, Pallas kernels, body(): pl.pallas_call(finish_kernel, out_shape=jax.ShapeDtypeStruct((width, colu...  3.45 us

profile of v6, /device:TPU:1, one launch (start us, length us, event | category | flops | bytes accessed | tf_op | source)
XLA Modules:
  0.0 143.7 jit_solution(16455647567081150256)
XLA Ops:
  0.0 140.2 %shard_map.46 = (bf16[2048,256]{1,0:T(8,128)(2,1)S(1)}, bf16[1024,2048]{1,0:T(8,128)(2,1)S(1)}, bf16[2,1024,1024]{2,1,0:T(8,128)(2,1)S(1)}, bf16[2048,1024]{1,0:T(8,128)(2,1)S(1)}, f32[2048,1024]{1,0:T(8,128)S(1)}) custom-call(bf16[256,2048]{1,0:T(8,128)(2,1)} %tok_ref.1, bf16[256,8192]{1,0:T(8,128)(2,1)} %cot_ref.1, bf16[2048,2048]{1,0:T(8,128)(2,1)} %bitcast.3, ...), custom_call_target="tpu_custom_call" | custom-call | tf_op jit(solution)/shard_map/pallas_call | solution.py:427
  140.2 3.4 %shard_map.47 = bf16[2048,2048]{1,0:T(8,128)(2,1)} custom-call(bf16[2048,256]{1,0:T(8,128)(2,1)S(1)} %get-tuple-element.10.x_ref, bf16[1024,2048]{1,0:T(8,128)(2,1)S(1)} %get-tuple-element.11.cot_ref, bf16[2,1024,1024]{2,1,0:T(8,128)(2,1)S(1)} %get-tuple-element.12.right_ref, bf16[2048,1024]{1,0:T(8,128)(2,1)S(1)} %get-tuple-element.13.done_ref, ...), custom_call_target="tpu_custom_call" | custom-call | tf_op jit(solution)/shard_map/pallas_call | solution.py:450
